TPU v7x, 32 devices: a whole 2x2x4 slice. The times are simulated.
32 devices in a mesh: mesh: 8 (over z, x), col: 4 (over y, core).
Axes of the slice: x: 2, y: 2, z: 4, core: 2. Of those that a mesh axis runs over, the one named last changes fastest.
Arguments:
- x_cols: bfloat16 [32, 8192], P('col', 'mesh'), may hold values from -6 to 6
- q_tiles: bfloat16 [320, 128, 128], P('mesh'), may hold values from -0.25 to 0.25
- q_cols: int32 [64, 5], P('mesh'), may hold values from 0 to 15, as said below
- halo_ids: int32 [8, 2], P('mesh'), may hold values from 0 to 7
- a_tiles: bfloat16 [512, 128, 128], P('mesh'), may hold values from -0.1875 to 0.1875
- obs_prec: bfloat16 [512, 128], P('mesh'), may hold values from 0.5 to 4
- tile_owner: int32 [512, 1], P('mesh'), may hold values from 0 to 7; in each aligned block of 64 rows (0 to 63, 64 to 127, ...) at most 16 rows name the same one
- tile_sub: int32 [512], P('mesh'), may hold values from 0 to 7
Outputs:
- product: float32 [32, 8192], P('col', 'mesh')
- gram: float32 [32, 32], P(None, 'col')
Inputs may be any that keep to these rules, and one draw needn't show every extreme that they name: `q_cols`: slot values index a partition's window of 16 row blocks as the first step defines. `tile_owner`: among the 64 tiles of one partition, no partition is named more than 16 times.
All inputs are finite; a program needn't handle non-finite values.
Results may differ from a plain program's by a relative error of at most 0.00081.
Values may be sent and summed in bfloat16 or wider, within the bound.
No kernel may reach another device: no remote copies, remote signals or barrier semaphores. Data moves between devices by JAX's collectives and lax.ppermute only.
A program may use at most 64 MiB of HBM per device.

v0:
```python
import math

import jax
import jax.numpy as jnp
from jax import lax
from jax.sharding import PartitionSpec as P

HIGHEST = lax.Precision.HIGHEST


def passed_along(array, axis, by):
    length = lax.axis_size(axis)
    return lax.ppermute(array, axis, [(i, (i + by) % length) for i in range(length)])


def tile_terms(obs_tiles, precisions, x_tiles):
    projected = jnp.einsum("ton,tcn->tco", obs_tiles, x_tiles, preferred_element_type=jnp.float32)
    weighted = (precisions.astype(jnp.float32)[:, None, :] * projected).astype(jnp.bfloat16)
    return jnp.einsum("ton,tco->tcn", obs_tiles, weighted, preferred_element_type=jnp.float32)


def body(x_cols, q_tiles, q_cols, halo_ids, a_tiles, obs_prec, tile_owner, tile_sub):
    col_width, local_nodes = x_cols.shape
    tile_size = a_tiles.shape[1]
    row_blocks = local_nodes // tile_size
    neighbours = q_cols.shape[1]
    mesh_parts = lax.axis_size("mesh")
    obs_count = a_tiles.shape[0]
    capacity = max(2, 2 * obs_count // mesh_parts)
    slot_count = mesh_parts * capacity
    tile_total = row_blocks * neighbours
    probes = lax.all_gather(x_cols, "col", axis=0, tiled=True)
    blocks = x_cols.reshape(col_width, row_blocks, tile_size).transpose(1, 0, 2)
    block_ids = jnp.arange(row_blocks, dtype=jnp.int32)
    picker = (block_ids[None, :] == halo_ids[0][:, None]).astype(jnp.bfloat16)
    shared = jnp.einsum("hr,rcn->hcn", picker, blocks, preferred_element_type=jnp.float32).astype(
        jnp.bfloat16
    )
    left_far = passed_along(shared, "mesh", 2)
    left_near = passed_along(shared, "mesh", 1)
    right_near = passed_along(shared, "mesh", -1)
    right_far = passed_along(shared, "mesh", -2)
    window = jnp.concatenate([blocks, left_far, left_near, right_near, right_far], axis=0)
    slot_list = q_cols.reshape(-1)
    chosen = jnp.take(window, slot_list, axis=0)
    tile_products = jnp.einsum("kij,kcj->kci", q_tiles, chosen, preferred_element_type=jnp.float32)
    tile_rows = jnp.arange(tile_total, dtype=jnp.int32) // neighbours
    row_map = (block_ids[:, None] == tile_rows[None, :]).astype(jnp.float32)
    prior_part = jnp.einsum("rk,kcn->rcn", row_map, tile_products, precision=HIGHEST)
    owners = tile_owner[:, 0]
    positions = jnp.arange(obs_count, dtype=jnp.int32)
    earlier = (owners[:, None] == owners[None, :]) & (positions[None, :] < positions[:, None])
    rank_of = jnp.sum(earlier.astype(jnp.int32), axis=1)
    slot_of = owners * capacity + rank_of
    slot_ids = jnp.arange(slot_count, dtype=jnp.int32)
    placed = slot_ids[:, None] == slot_of[None, :]
    asked_ids = jnp.sum(jnp.where(placed, tile_sub[None, :] + 1, 0), axis=1) - 1
    source_tile = jnp.sum(jnp.where(placed, positions[None, :], 0), axis=1)
    incoming = lax.all_to_all(asked_ids, "mesh", split_axis=0, concat_axis=0, tiled=True)
    landing = block_ids[:, None] == incoming[None, :]
    answer = jnp.einsum(
        "rs,rcn->scn", landing.astype(jnp.bfloat16), blocks, preferred_element_type=jnp.float32
    ).astype(jnp.bfloat16)
    x_tiles = lax.all_to_all(answer, "mesh", split_axis=0, concat_axis=0, tiled=True)
    sent_terms = tile_terms(
        jnp.take(a_tiles, source_tile, axis=0), jnp.take(obs_prec, source_tile, axis=0), x_tiles
    )
    slot_terms = lax.all_to_all(sent_terms, "mesh", split_axis=0, concat_axis=0, tiled=True)
    observed = jnp.einsum("rs,scn->rcn", landing.astype(jnp.float32), slot_terms, precision=HIGHEST)
    combined = prior_part + observed
    y_local = combined.transpose(1, 0, 2).reshape(col_width, local_nodes)
    partial_value = jnp.dot(probes.astype(jnp.float32), y_local.T, precision=HIGHEST)
    total_nodes = local_nodes * mesh_parts
    gram_block = lax.psum(partial_value, "mesh") / math.sqrt(total_nodes)
    return (y_local, gram_block)


def solution(mesh):
    placed = (
        P("col", "mesh"),
        P("mesh", None, None),
        P("mesh", None),
        P("mesh", None),
        P("mesh", None, None),
        P("mesh", None),
        P("mesh", None),
        P("mesh"),
    )
    return jax.shard_map(
        body,
        mesh=mesh,
        in_specs=placed,
        out_specs=(P("col", "mesh"), P(None, "col")),
        check_vma=False,
    )
```

profile of v0, /device:TPU:0, one launch (start us, length us, event | category | flops | bytes accessed | tf_op | source)
XLA Modules:
  0.0 86.1 jit_solution(6876523231642189622)
XLA Ops:
  0.6 0.0 copy-start
  0.6 1.1 %convolution_convert_fusion.1 = bf16[2,8,128]{2,0,1:T(2,128)(2,1)S(1)} fusion(bf16[8,8,128]{2,1,0:T(8,128)(2,1)} %bitcast.37, s32[2]{0:T(128)} %bitcast.42), kind=kOutput, calls=%fused_computation.11 | convolution fusion | flops 34832 | bytes 20488 | tf_op jit(solution)/shard_map/hr,rcn->hcn/dot_general | solution.py:36
  1.7 3.1 %collective-permute-start = (bf16[2,8,128]{2,0,1:T(2,128)(2,1)S(1)}, bf16[2,8,128]{2,0,1:T(2,128)(2,1)S(1)}, u32[]{:S(2)}, u32[]{:S(2)}) collective-permute-start(bf16[2,8,128]{2,0,1:T(2,128)(2,1)S(1)} %convolution_convert_fusion.1), channel_id=1, source_target_pairs={{0,8},{4,12},{8,16},{12,20},{16,24},{20,28},{24,0},{28,4},{1,9},{5... | collective-permute-start | bytes 12296 | tf_op jit(solution)/shard_map/ppermute | solution.py:13
  4.8 1.5 %collective-permute-start.1 = (bf16[2,8,128]{2,0,1:T(2,128)(2,1)S(1)}, bf16[2,8,128]{2,0,1:T(2,128)(2,1)S(1)}, u32[]{:S(2)}, u32[]{:S(2)}) collective-permute-start(bf16[2,8,128]{2,0,1:T(2,128)(2,1)S(1)} %convolution_convert_fusion.1), channel_id=1, source_target_pairs={{0,4},{4,8},{8,12},{12,16},{16,20},{20,24},{24,28},{28,0},{1,5},{5... | collective-permute-start | bytes 12296 | tf_op jit(solution)/shard_map/ppermute | solution.py:13
  6.3 3.2 %collective-permute-start.2 = (bf16[2,8,128]{2,0,1:T(2,128)(2,1)S(1)}, bf16[2,8,128]{2,0,1:T(2,128)(2,1)S(1)}, u32[]{:S(2)}, u32[]{:S(2)}) collective-permute-start(bf16[2,8,128]{2,0,1:T(2,128)(2,1)S(1)} %convolution_convert_fusion.1), channel_id=1, source_target_pairs={{0,28},{4,0},{8,4},{12,8},{16,12},{20,16},{24,20},{28,24},{1,29},{... | collective-permute-start | bytes 12296 | tf_op jit(solution)/shard_map/ppermute | solution.py:13
  9.5 0.3 collective-permute-start.3
  9.8 0.9 %convert_reduce_fusion = s32[64]{0:T(128)S(1)} fusion(s32[64]{0:T(128)} %bitcast.41), kind=kLoop, calls=%fused_computation.25 | loop fusion | flops 20416 | bytes 512 | tf_op jit(solution)/shard_map/reduce_sum | solution.py:53
  10.7 0.7 multiply_add_fusion
  11.4 0.1 select_reduce_fusion.1
  11.5 0.7 sub.14
  12.1 3.3 %all-to-all-start = ((s32[8,16,1]{1,2,0:T(1,128)}), s32[8,16,1]{1,2,0:T(1,128)S(1)}, u32[]{:S(2)}, u32[]{:S(2)}) async-start(s32[8,16,1]{1,2,0:T(1,128)} %bitcast.8), calls=%async_computation | async-start | bytes 8192 | tf_op jit(solution)/shard_map/all_to_all | solution.py:59
  15.5 0.7 constant_dynamic-update-slice_fusion.4
  16.2 0.8 reshape.123
  17.0 0.8 reshape.121
  17.8 1.4 %gather_fusion.1 = bf16[128,128]{1,0:T(8,128)(2,1)S(1)} fusion(bf16[64,128]{1,0:T(8,128)(2,1)} %param.13, s32[1024]{0:T(1024)S(1)} %pad_clamp_fusion), kind=kCustom, calls=%fused_computation.1 | custom fusion | bytes 66048 | tf_op jit(solution)/shard_map/jit(_take)/gather | solution.py:66
  19.2 0.1 select_convert_fusion
  19.3 2.6 %all-to-all-done = s32[8,16,1]{1,2,0:T(1,128)S(1)} async-done(((s32[8,16,1]{1,2,0:T(1,128)}), s32[8,16,1]{1,2,0:T(1,128)S(1)}, u32[]{:S(2)}, u32[]{:S(2)}) %all-to-all-start) | async-done | bytes 544 | tf_op jit(solution)/shard_map/all_to_all | solution.py:59
  21.8 0.5 broadcast.118
  22.4 0.7 reduce.3
  23.0 0.1 eq.83
  23.1 1.0 %convolution_convert_fusion = bf16[128,8,128]{2,0,1:T(8,128)(2,1)S(1)} fusion(bf16[8,8,128]{2,1,0:T(8,128)(2,1)} %bitcast.38, s32[128]{0:T(128)S(1)} %eq.83), kind=kOutput, calls=%fused_computation.8 | convolution fusion | flops 2229248 | bytes 279040 | tf_op jit(solution)/shard_map/rs,rcn->scn/dot_general | solution.py:61
  24.1 0.9 copy.44
  25.0 3.4 %all-to-all-start.1 = ((bf16[128,8,128]{2,1,0:T(8,128)(2,1)}), bf16[128,8,128]{2,1,0:T(8,128)(2,1)S(1)}, u32[]{:S(2)}, u32[]{:S(2)}) async-start(bf16[128,8,128]{2,1,0:T(8,128)(2,1)} %copy.44), calls=%async_computation.1 | async-start | bytes 524288 | tf_op jit(solution)/shard_map/all_to_all | solution.py:64
  28.4 5.4 %all_gather.3 = bf16[32,1024]{1,0:T(8,128)(2,1)S(1)} all-gather(bf16[8,1024]{1,0:T(8,128)(2,1)} %param.8), channel_id=1, replica_groups=mesh['mesh'=8,'col'=4] {'col'}, dimensions={0}, use_global_device_ids=true | all-gather | bytes 81920 | tf_op jit(solution)/shard_map/all_gather | solution.py:32
  33.8 0.0 copy-done
  33.8 3.0 %gather_fusion.2 = bf16[128,128,128]{2,1,0:T(8,128)(2,1)} fusion(bf16[64,128,128]{2,1,0:T(8,128)(2,1)S(1)} %copy-done, s32[1024]{0:T(1024)S(1)} %pad_clamp_fusion), kind=kCustom, calls=%fused_computation.2 | custom fusion | bytes 8389120 | tf_op jit(solution)/shard_map/jit(_take)/gather | solution.py:66
  36.8 0.0 collective-permute-done
  36.9 0.0 collective-permute-done.1
  36.9 0.0 all-to-all-done.1
  36.9 7.7 %fusion = f32[128,8,128]{2,1,0:T(8,128)} fusion(bf16[128,128,128]{2,1,0:T(8,128)(2,1)} %gather_fusion.2, pred[128]{0:T(512)(128)(4,1)S(1)} %compare_and_fusion, bf16[128,8,128]{2,1,0:T(8,128)(2,1)S(1)} %all-to-all-done.1, f32[128,128]{1,0:T(8,128)S(1)} %select_convert_fusion), kind=kOutput, calls=%fused_computation.4 | convolution fusion | flops 71565312 | bytes 5046400 | tf_op jit(solution)/shard_map/ton,tco->tcn/dot_general | solution.py:19
  44.6 6.0 %all-to-all-start.2 = ((f32[128,8,128]{2,1,0:T(8,128)}), f32[128,8,128]{2,1,0:T(8,128)S(1)}, u32[]{:S(2)}, u32[]{:S(2)}) async-start(f32[128,8,128]{2,1,0:T(8,128)} %fusion), calls=%async_computation.2 | async-start | bytes 1048576 | tf_op jit(solution)/shard_map/all_to_all | solution.py:68
  50.5 0.0 collective-permute-done.2
  50.6 0.0 collective-permute-done.3
  50.6 0.6 gather_fusion
  51.2 2.1 %fusion.9 = f32[40,8,128]{2,1,0:T(8,128)S(1)} fusion(bf16[40,128,128]{2,1,0:T(8,128)(2,1)} %param.9, bf16[40,8,128]{2,1,0:T(8,128)(2,1)S(1)} %gather_fusion, pred[40]{0:T(512)(128)(4,1)S(1)} %compare_and_fusion.1), kind=kOutput, calls=%fused_computation.17 | convolution fusion | flops 10526720 | bytes 1556520 | tf_op jit(solution)/shard_map/kij,kcj->kci/dot_general | solution.py:46
  53.3 0.2 fusion.7
  53.5 12.0 %all-to-all-done.2 = f32[128,8,128]{2,1,0:T(8,128)S(1)} async-done(((f32[128,8,128]{2,1,0:T(8,128)}), f32[128,8,128]{2,1,0:T(8,128)S(1)}, u32[]{:S(2)}, u32[]{:S(2)}) %all-to-all-start.2) | async-done | bytes 524320 | tf_op jit(solution)/shard_map/all_to_all | solution.py:68
  65.5 0.3 fusion.4
  65.9 0.0 copy-start.1
  65.9 0.1 convolution_bitcast_fusion
  66.0 19.5 %psum.7 = f32[32,8]{0,1:T(8,128)S(1)} all-reduce(f32[32,8]{0,1:T(8,128)S(1)} %convolution_bitcast_fusion), channel_id=1, replica_groups=mesh['mesh'=8,'col'=4] {'mesh'}, use_global_device_ids=true, to_apply=%region_3.4 | all-reduce | flops 256 | bytes 2048 | tf_op jit(solution)/shard_map/psum | solution.py:74
  85.5 0.6 broadcast_multiply_fusion
  86.1 0.0 copy-done.1
  (13 shorter events, 0.1 us)
Async XLA Ops:
  0.6 33.2 %copy-start = (bf16[64,128,128]{2,1,0:T(8,128)(2,1)S(1)}, bf16[64,128,128]{2,1,0:T(8,128)(2,1)}, u32[]{:S(2)}) copy-start(bf16[64,128,128]{2,1,0:T(8,128)(2,1)} %param.12) | copy-start | bytes 6291460
  1.7 35.1 %collective-permute-start = (bf16[2,8,128]{2,0,1:T(2,128)(2,1)S(1)}, bf16[2,8,128]{2,0,1:T(2,128)(2,1)S(1)}, u32[]{:S(2)}, u32[]{:S(2)}) collective-permute-start(bf16[2,8,128]{2,0,1:T(2,128)(2,1)S(1)} %convolution_convert_fusion.1), channel_id=1, source_target_pairs={{0,8},{4,12},{8,16},{12,20},{16,24},{20,28},{24,0},{28,4},{1,9},{5... | collective-permute-start | bytes 12296 | tf_op jit(solution)/shard_map/ppermute | solution.py:13
  4.8 32.1 %collective-permute-start.1 = (bf16[2,8,128]{2,0,1:T(2,128)(2,1)S(1)}, bf16[2,8,128]{2,0,1:T(2,128)(2,1)S(1)}, u32[]{:S(2)}, u32[]{:S(2)}) collective-permute-start(bf16[2,8,128]{2,0,1:T(2,128)(2,1)S(1)} %convolution_convert_fusion.1), channel_id=1, source_target_pairs={{0,4},{4,8},{8,12},{12,16},{16,20},{20,24},{24,28},{28,0},{1,5},{5... | collective-permute-start | bytes 12296 | tf_op jit(solution)/shard_map/ppermute | solution.py:13
  6.3 44.3 %collective-permute-start.2 = (bf16[2,8,128]{2,0,1:T(2,128)(2,1)S(1)}, bf16[2,8,128]{2,0,1:T(2,128)(2,1)S(1)}, u32[]{:S(2)}, u32[]{:S(2)}) collective-permute-start(bf16[2,8,128]{2,0,1:T(2,128)(2,1)S(1)} %convolution_convert_fusion.1), channel_id=1, source_target_pairs={{0,28},{4,0},{8,4},{12,8},{16,12},{20,16},{24,20},{28,24},{1,29},{... | collective-permute-start | bytes 12296 | tf_op jit(solution)/shard_map/ppermute | solution.py:13
  9.5 41.1 %collective-permute-start.3 = (bf16[2,8,128]{2,0,1:T(2,128)(2,1)S(1)}, bf16[2,8,128]{2,0,1:T(2,128)(2,1)S(1)}, u32[]{:S(2)}, u32[]{:S(2)}) collective-permute-start(bf16[2,8,128]{2,0,1:T(2,128)(2,1)S(1)} %convolution_convert_fusion.1), channel_id=1, source_target_pairs={{0,24},{4,28},{8,0},{12,4},{16,8},{20,12},{24,16},{28,20},{1,25},{... | collective-permute-start | bytes 12296 | tf_op jit(solution)/shard_map/ppermute | solution.py:13
  12.1 9.7 %all-to-all-start = ((s32[8,16,1]{1,2,0:T(1,128)}), s32[8,16,1]{1,2,0:T(1,128)S(1)}, u32[]{:S(2)}, u32[]{:S(2)}) async-start(s32[8,16,1]{1,2,0:T(1,128)} %bitcast.8), calls=%async_computation | async-start | bytes 8192 | tf_op jit(solution)/shard_map/all_to_all | solution.py:59
  25.0 11.9 %all-to-all-start.1 = ((bf16[128,8,128]{2,1,0:T(8,128)(2,1)}), bf16[128,8,128]{2,1,0:T(8,128)(2,1)S(1)}, u32[]{:S(2)}, u32[]{:S(2)}) async-start(bf16[128,8,128]{2,1,0:T(8,128)(2,1)} %copy.44), calls=%async_computation.1 | async-start | bytes 524288 | tf_op jit(solution)/shard_map/all_to_all | solution.py:64
  44.6 20.9 %all-to-all-start.2 = ((f32[128,8,128]{2,1,0:T(8,128)}), f32[128,8,128]{2,1,0:T(8,128)S(1)}, u32[]{:S(2)}, u32[]{:S(2)}) async-start(f32[128,8,128]{2,1,0:T(8,128)} %fusion), calls=%async_computation.2 | async-start | bytes 1048576 | tf_op jit(solution)/shard_map/all_to_all | solution.py:68
  65.9 20.2 %copy-start.1 = (f32[1,8,8,128]{3,1,2,0:T(8,128)}, f32[1,8,8,128]{3,1,2,0:T(8,128)S(1)}, u32[]{:S(2)}) copy-start(f32[1,8,8,128]{3,1,2,0:T(8,128)S(1)} %copy.60) | copy-start | bytes 98308
where the time goes:
time: 86.9 us; the launch traced here: 86.1 us
  blocking collectives  25 us (29%)
  starting transfers between devices  20.7 us (24%)
  waiting for transfers between devices  14.6 us (17%)
  matrix products  12.5 us (14%)
  local copies, waits for them, and re-layouts  9.44 us (11%)
  other arithmetic  3.08 us (4%)
    psum x1, blocking collectives, body(): gram_block = lax.psum(partial_value, 'mesh') / math.sqrt(total_nodes)  19.5 us
    all_to_all x1, waiting for transfers between devices, body(): lax.all_to_all(sent_terms, 'mesh', split_axis=0, concat_axis=0, tiled=True)  12 us
    ppermute x4, starting transfers between devices, passed_along(): lax.ppermute(array, axis, [(i, (i + by) % length) for i in range(length)])  8.04 us
    dot_general x1, matrix products, tile_terms(): jnp.einsum('ton,tco->tcn', obs_tiles, weighted, preferred_element_type=jn...  7.69 us
    all_to_all x1, starting transfers between devices, body(): lax.all_to_all(sent_terms, 'mesh', split_axis=0, concat_axis=0, tiled=True)  5.95 us
    all_gather x1, blocking collectives, body(): probes = lax.all_gather(x_cols, 'col', axis=0, tiled=True)  5.45 us
    all_to_all x1, starting transfers between devices, body(): lax.all_to_all(answer, 'mesh', split_axis=0, concat_axis=0, tiled=True)  3.41 us
    all_to_all x1, starting transfers between devices, body(): lax.all_to_all(asked_ids, 'mesh', split_axis=0, concat_axis=0, tiled=True)  3.31 us
  transfers between devices with their start and end apart: 7, of which 2 were waited for; matrix products, arithmetic and copies ran while one was open for 27% of the time, Pallas kernels for 0%

commit v1 on v0

v1 whole, which is shorter than its diff:
```python
import math

import jax
import jax.numpy as jnp
from jax import lax
from jax.experimental import pallas as pl
from jax.experimental.pallas import tpu as pltpu
from jax.sharding import PartitionSpec as P

OFFSETS = (-2, -1, 1, 2)
LANES = 128
NT = (((1,), (1,)), ((), ()))
UNROLL = 16
GRANT = 16 * 2**20


def offer_kernel(halo_ids, x_cols, offered):
    parts, cols, width = offered.shape
    nodes = width - LANES
    rows = lax.broadcasted_iota(jnp.int32, (cols, LANES), 0)
    ids = jnp.zeros((cols, LANES), jnp.float32)
    for j in range(halo_ids.shape[1]):
        ids = jnp.where(rows == j, halo_ids[0, j].astype(jnp.float32), ids)
    ids = ids.astype(offered.dtype)
    own = x_cols[...]

    def put(part, carry):
        offered[part, :, :nodes] = own
        offered[part, :, nodes:] = ids
        return carry

    lax.fori_loop(0, parts, put, 0)


def terms_kernel(
    owners, subs, q_cols, xg, a_tiles, precisions, q_tiles, message, window, weighted
):
    parts, cols, width = xg.shape
    obs_count, tile, _ = a_tiles.shape
    row_blocks, neighbours = q_cols.shape
    nodes = row_blocks * tile
    halo = (window.shape[0] - row_blocks) // len(OFFSETS)
    me = lax.axis_index("mesh")

    def block(part, row):
        return xg[part, :, pl.ds(pl.multiple_of(row * tile, tile), tile)]

    for row in range(row_blocks):
        window[row] = xg[me, :, row * tile:(row + 1) * tile]
    for m, offset in enumerate(OFFSETS):
        part = lax.rem(me + offset + parts, parts)
        ids = xg[part, :, nodes:nodes + tile].astype(jnp.float32)
        for j in range(halo):
            wanted = jnp.broadcast_to(ids[j:j + 1, :], (cols, tile))
            picked = jnp.zeros((cols, tile), jnp.float32)
            for row in range(row_blocks):
                picked = jnp.where(
                    wanted == float(row),
                    xg[part, :, row * tile:(row + 1) * tile].astype(jnp.float32),
                    picked,
                )
            window[row_blocks + m * halo + j] = picked.astype(jnp.bfloat16)

    message[...] = jnp.zeros_like(message)

    def project(step, carry):
        first = pl.multiple_of(step * UNROLL, UNROLL)
        scales = precisions[pl.ds(first, UNROLL), :].astype(jnp.float32)
        for u in range(UNROLL):
            t = step * UNROLL + u
            projected = lax.dot_general(
                block(owners[t], subs[t]), a_tiles[t], NT, preferred_element_type=jnp.float32
            )
            weighted[t] = (scales[u:u + 1, :] * projected).astype(jnp.bfloat16)
        return carry

    lax.fori_loop(0, obs_count // UNROLL, project, 0)

    for row in range(row_blocks):
        total = None
        for k in range(neighbours):
            term = lax.dot_general(
                window[q_cols[row, k]], q_tiles[row * neighbours + k], NT,
                preferred_element_type=jnp.float32,
            )
            total = term if total is None else total + term
        message[me, :, row * tile:(row + 1) * tile] = total

    def spread(step, carry):
        made = [
            jnp.dot(weighted[step * UNROLL + u], a_tiles[step * UNROLL + u],
                    preferred_element_type=jnp.float32)
            for u in range(UNROLL)
        ]
        for u in range(UNROLL):
            t = step * UNROLL + u
            lanes = pl.ds(pl.multiple_of(subs[t] * tile, tile), tile)
            message[owners[t], :, lanes] = message[owners[t], :, lanes] + made[u]
        return carry

    lax.fori_loop(0, obs_count // UNROLL, spread, 0)


def gram_kernel(sent, own, near1, near2, near3, message):
    parts, cols, width = own.shape
    nodes = width - LANES
    mine = lax.axis_index("col")
    total = jnp.zeros((cols, LANES), jnp.float32)
    pieces = [None] * 4

    def add(part, carry):
        value = sent[part, :, :nodes]
        high = value.astype(jnp.bfloat16)
        low = (value - high.astype(jnp.float32)).astype(jnp.bfloat16)
        out = []
        for ref, old in zip((own, near1, near2, near3), carry):
            x = ref[part, :, :nodes]
            out.append(
                old
                + lax.dot_general(high, x, NT, preferred_element_type=jnp.float32)
                + lax.dot_general(low, x, NT, preferred_element_type=jnp.float32)
            )
        return tuple(out)

    pieces = tuple(jnp.zeros((cols, cols), jnp.float32) for _ in range(4))
    if parts <= 16:
        for part in range(parts):
            pieces = add(part, pieces)
    else:
        pieces = lax.fori_loop(0, parts, add, pieces)
    for k, piece in enumerate(pieces):
        wide = jnp.concatenate([piece, jnp.zeros((cols, LANES - cols), jnp.float32)], axis=1)
        total = total + pltpu.roll(wide, lax.bitwise_xor(mine, k) * cols, 1)

    def put(part, carry):
        message[part, :, nodes:] = total
        return carry

    lax.fori_loop(0, parts, put, 0)


def body(x_cols, q_tiles, q_cols, halo_ids, a_tiles, obs_prec, tile_owner, tile_sub):
    cols, nodes = x_cols.shape
    parts, groups = lax.axis_size("mesh"), lax.axis_size("col")
    obs_count, tile, _ = a_tiles.shape
    row_blocks = nodes // tile
    halo = halo_ids.shape[1]
    width = nodes + LANES
    vmem, smem = pl.BlockSpec(memory_space=pltpu.VMEM), pl.BlockSpec(memory_space=pltpu.SMEM)
    offered = pl.pallas_call(
        offer_kernel,
        out_shape=jax.ShapeDtypeStruct((parts, cols, width), x_cols.dtype),
        in_specs=[smem, vmem],
        out_specs=vmem,
        compiler_params=pltpu.CompilerParams(vmem_limit_bytes=GRANT),
        name="offer",
    )(halo_ids, x_cols)
    xg = lax.all_to_all(offered, "mesh", 0, 0, tiled=True)
    near = [
        lax.ppermute(xg, "col", [(i, i ^ k) for i in range(groups)]) for k in range(1, groups)
    ]
    shape = jax.ShapeDtypeStruct((parts, cols, width), jnp.float32)
    message = pl.pallas_call(
        terms_kernel,
        out_shape=shape,
        in_specs=[smem, smem, smem, vmem, vmem, vmem, vmem],
        out_specs=vmem,
        scratch_shapes=[
            pltpu.VMEM((row_blocks + len(OFFSETS) * halo, cols, tile), jnp.bfloat16),
            pltpu.VMEM((obs_count, cols, tile), jnp.bfloat16),
        ],
        cost_estimate=pl.CostEstimate(
            flops=60_000_000, bytes_accessed=4_000_000, transcendentals=0
        ),
        compiler_params=pltpu.CompilerParams(vmem_limit_bytes=GRANT),
        name="terms",
    )(tile_owner.reshape(-1), tile_sub, q_cols, xg, a_tiles, obs_prec, q_tiles)
    message = pl.pallas_call(
        gram_kernel,
        out_shape=shape,
        in_specs=[vmem] * 5,
        out_specs=vmem,
        input_output_aliases={0: 0},
        cost_estimate=pl.CostEstimate(
            flops=10_000_000, bytes_accessed=1_000_000, transcendentals=0
        ),
        compiler_params=pltpu.CompilerParams(vmem_limit_bytes=GRANT),
        name="gram",
    )(message, xg, *near)
    arrived = lax.all_to_all(message, "mesh", 0, 0, tiled=True)
    summed = jnp.sum(arrived, axis=0)
    gram = summed[:, nodes:nodes + groups * cols].T / math.sqrt(nodes * parts)
    return summed[:, :nodes], gram


def solution(mesh):
    placed = (
        P("col", "mesh"),
        P("mesh", None, None),
        P("mesh", None),
        P("mesh", None),
        P("mesh", None, None),
        P("mesh", None),
        P("mesh", None),
        P("mesh"),
    )
    return jax.shard_map(
        body,
        mesh=mesh,
        in_specs=placed,
        out_specs=(P("col", "mesh"), P(None, "col")),
        check_vma=False,
    )
```

time: 86.9 us -> 44.6 us (0.51)
  starting transfers between devices: 20.7 us -> 1.86 us
  waiting for transfers between devices: 14.6 us -> 0.01 us
  matrix products: 12.5 us -> 0 us
  Pallas kernels: 0 us -> 5.49 us
  blocking collectives: 25 us -> 27.9 us
  other arithmetic: 3.08 us -> 0.62 us
  local copies, waits for them, and re-layouts: 9.44 us -> 7.6 us
    all_to_all x0 -> x2, blocking collectives: none -> 27.9 us  [the longest x1 14.5 us: body(): xg = lax.all_to_all(offered, 'mesh', 0, 0, tiled=True)]
    psum x1 -> x0, blocking collectives: 19.5 us -> none  [body(): gram_block = lax.psum(partial_value, 'mesh') / math.sqrt(total_nodes)]
    all_to_all x3 -> x0, waiting for transfers between devices: 14.6 us -> none  [the longest x1 12 us: body(): lax.all_to_all(sent_terms, 'mesh', split_axis=0, concat_axis=0, tiled=True)]
    all_to_all x3 -> x0, starting transfers between devices: 12.7 us -> none  [the longest x1 5.95 us: body(): lax.all_to_all(sent_terms, 'mesh', split_axis=0, concat_axis=0, tiled=True)]
    dot_general x7 -> x0, matrix products: 12.5 us -> none  [the longest x1 7.69 us: tile_terms(): jnp.einsum('ton,tco->tcn', obs_tiles, weighted, preferred_element_type=jn...]
    unnamed x9 -> x16, local copies, waits for them, and re-layouts: 0.78 us -> 6.98 us
    ppermute x4 -> x3, starting transfers between devices: 8.04 us -> 1.86 us  [body(): lax.ppermute(xg, 'col', [(i, i ^ k) for i in range(groups)])]
    pallas_call x0 -> x3, Pallas kernels: none -> 5.49 us  [the longest x1 3.93 us: body(): pl.pallas_call(terms_kernel, out_shape=shape, in_specs=[smem, smem, smem,...]
  transfers between devices with their start and end apart: 7 -> 3, of which waited for: 2 -> 0; matrix products, arithmetic and copies ran while one was open for 27% -> 0% of each run, Pallas kernels for 0% -> 9%
where the time goes in v1:
time: 44.6 us; the launch traced here: 44.1 us
  blocking collectives  27.9 us (63%)
  local copies, waits for them, and re-layouts  7.6 us (17%)
  Pallas kernels  5.49 us (12%)
  starting transfers between devices  1.86 us (4%)
  between operations  0.68 us (2%)
  other arithmetic  0.62 us (1%)
    all_to_all x1, blocking collectives, body(): xg = lax.all_to_all(offered, 'mesh', 0, 0, tiled=True)  14.5 us
    all_to_all x1, blocking collectives, body(): arrived = lax.all_to_all(message, 'mesh', 0, 0, tiled=True)  13.4 us
    unnamed x16, local copies, waits for them, and re-layouts  6.98 us
    pallas_call x1, Pallas kernels, body(): pl.pallas_call(terms_kernel, out_shape=shape, in_specs=[smem, smem, smem,...  3.93 us
    ppermute x3, starting transfers between devices, body(): lax.ppermute(xg, 'col', [(i, i ^ k) for i in range(groups)])  1.86 us
    pallas_call x1, Pallas kernels, body(): pl.pallas_call(gram_kernel, out_shape=shape, in_specs=[vmem] * 5, out_spe...  0.98 us
  transfers between devices with their start and end apart: 3, of which 0 were waited for; matrix products, arithmetic and copies ran while one was open for 0% of the time, Pallas kernels for 9%

profile of v1, /device:TPU:0, one launch (start us, length us, event | category | flops | bytes accessed | tf_op | source)
XLA Modules:
  0.0 44.1 jit_solution(8727041809188360824)
XLA Ops:
  0.6 0.0 copy-start.3
  0.6 0.7 %copy-done.3 = bf16[8,1024]{1,0:T(8,128)(2,1)S(1)} copy-done((bf16[8,1024]{1,0:T(8,128)(2,1)S(1)}, bf16[8,1024]{1,0:T(8,128)(2,1)}, u32[]{:S(2)}) %copy-start.3) | copy-done | bytes 16408
  1.3 0.0 copy-start.5
  1.4 0.7 %copy-done.5 = s32[1,2]{1,0:T(1,128)S(1)} copy-done((s32[1,2]{1,0:T(1,128)S(1)}, s32[1,2]{1,0:T(1,128)}, u32[]{:S(2)}) %copy-start.5) | copy-done | bytes 32
  2.0 0.6 %offer.1 = bf16[8,8,1152]{2,1,0:T(8,128)(2,1)S(1)} custom-call(s32[1,2]{1,0:T(1,128)S(1)} %copy-done.5, bf16[8,1024]{1,0:T(8,128)(2,1)S(1)} %copy-done.3), custom_call_target="tpu_custom_call" | custom-call | tf_op jit(solution)/shard_map/offer/pallas_call | solution.py:150
  2.6 14.5 %all_to_all.10.xg.own = bf16[8,8,1152]{2,1,0:T(8,128)(2,1)S(1)} all-to-all(bf16[8,8,1152]{2,1,0:T(8,128)(2,1)S(1)} %offer.1), channel_id=1, replica_groups=mesh['mesh'=8,'col'=4] {'mesh'}, dimensions={0} | all-to-all | bytes 294912 | tf_op jit(solution)/shard_map/all_to_all | solution.py:158
  17.1 0.0 collective-permute-start.2
  17.1 1.5 %collective-permute-start.1 = (bf16[8,8,1152]{2,1,0:T(8,128)(2,1)S(1)}, bf16[8,8,1152]{2,1,0:T(8,128)(2,1)S(1)}, u32[]{:S(2)}, u32[]{:S(2)}) collective-permute-start(bf16[8,8,1152]{2,1,0:T(8,128)(2,1)S(1)} %all_to_all.10.xg.own), channel_id=1, source_target_pairs={{0,2},{1,3},{2,0},{3,1},{4,6},{5,7},{6,4},{7,5},{8,10},{9,11},{10,... | collective-permute-start | bytes 442376 | tf_op jit(solution)/shard_map/ppermute | solution.py:160
  18.7 0.3 collective-permute-start
  19.0 0.0 copy-start
  19.0 1.6 %copy-done = bf16[64,128,128]{2,1,0:T(8,128)(2,1)S(1)} copy-done((bf16[64,128,128]{2,1,0:T(8,128)(2,1)S(1)}, bf16[64,128,128]{2,1,0:T(8,128)(2,1)}, u32[]{:S(2)}) %copy-start) | copy-done | bytes 2097176
  20.6 0.0 copy-start.1
  20.6 1.3 %copy-done.1 = bf16[40,128,128]{2,1,0:T(8,128)(2,1)S(1)} copy-done((bf16[40,128,128]{2,1,0:T(8,128)(2,1)S(1)}, bf16[40,128,128]{2,1,0:T(8,128)(2,1)}, u32[]{:S(2)}) %copy-start.1) | copy-done | bytes 1310744
  21.9 0.0 copy-start.2
  21.9 0.7 %copy-done.2 = bf16[64,128]{1,0:T(8,128)(2,1)S(1)} copy-done((bf16[64,128]{1,0:T(8,128)(2,1)S(1)}, bf16[64,128]{1,0:T(8,128)(2,1)}, u32[]{:S(2)}) %copy-start.2) | copy-done | bytes 16408
  22.6 0.0 copy-start.4
  22.6 0.7 %copy-done.4 = s32[8,5]{1,0:T(8,128)S(1)} copy-done((s32[8,5]{1,0:T(8,128)S(1)}, s32[8,5]{1,0:T(8,128)}, u32[]{:S(2)}) %copy-start.4) | copy-done | bytes 184
  23.3 0.0 copy-start.6
  23.3 0.7 %copy-done.6 = s32[64,1]{0,1:T(1,128)S(1)} copy-done((s32[64,1]{0,1:T(1,128)S(1)}, s32[64,1]{0,1:T(1,128)}, u32[]{:S(2)}) %copy-start.6) | copy-done | bytes 280
  24.0 0.0 copy-start.7
  24.0 0.7 %copy-done.7 = s32[64]{0:T(128)S(1)} copy-done((s32[64]{0:T(128)S(1)}, s32[64]{0:T(128)}, u32[]{:S(2)}) %copy-start.7) | copy-done | bytes 280
  24.6 3.9 %terms.1.sent = f32[8,8,1152]{2,1,0:T(8,128)S(1)} custom-call(s32[64]{0:T(128)S(1)} %bitcast.3, s32[64]{0:T(128)S(1)} %copy-done.7, s32[8,5]{1,0:T(8,128)S(1)} %copy-done.4, bf16[8,8,1152]{2,1,0:T(8,128)(2,1)S(1)} %all_to_all.10.xg.own, bf16[64,128,128]{2,1,0:T(8,128)(2,1)S(1)} %copy-done, bf16[64,128]{1,0:T(8,128)(2,1)S(1)} %copy-done.2, ...), custom_call_target="tpu_custom_call" | custom-call | flops 60000000 | bytes 4000000 | tf_op jit(solution)/shard_map/terms/pallas_call | solution.py:163
  28.5 0.0 collective-permute-done.2.near3
  28.6 0.0 collective-permute-done.1.near2
  28.6 0.0 collective-permute-done.near1
  28.6 1.0 %gram.1 = f32[8,8,1152]{2,1,0:T(8,128)S(1)} custom-call(f32[8,8,1152]{2,1,0:T(8,128)S(1)} %terms.1.sent, bf16[8,8,1152]{2,1,0:T(8,128)(2,1)S(1)} %all_to_all.10.xg.own, bf16[8,8,1152]{2,1,0:T(8,128)(2,1)S(1)} %collective-permute-done.near1, bf16[8,8,1152]{2,1,0:T(8,128)(2,1)S(1)} %collective-permute-done.1.near2, ...), custom_call_target="tpu_custom_call", output_to_operand_aliasing={{}: (0, {})} | custom-call | flops 10000000 | bytes 1000000 | tf_op jit(solution)/shard_map/gram/pallas_call | solution.py:178
  29.6 13.4 %all_to_all.11 = f32[8,8,1152]{2,1,0:T(8,128)S(1)} all-to-all(f32[8,8,1152]{2,1,0:T(8,128)S(1)} %gram.1), channel_id=1, replica_groups=mesh['mesh'=8,'col'=4] {'mesh'}, dimensions={0} | all-to-all | bytes 589824 | tf_op jit(solution)/shard_map/all_to_all | solution.py:190
  42.9 0.6 %fusion = f32[32,8]{0,1:T(8,128)} fusion(f32[8,1152]{1,0:T(8,128)S(1)} %reduce_sum.9), kind=kLoop, calls=%fused_computation.1 | loop fusion | flops 256 | bytes 2048 | tf_op jit(solution)/shard_map/div | solution.py:192
  43.5 0.6 %slice.8 = f32[8,1024]{1,0:T(8,128)} slice(f32[8,1152]{1,0:T(8,128)S(1)} %reduce_sum.9), slice={[0:8], [0:1024]} | slice | bytes 65536 | tf_op jit(solution)/shard_map/slice | solution.py:193
  (1 shorter events, 0.0 us)
Async XLA Ops:
  0.6 0.7 %copy-start.3 = (bf16[8,1024]{1,0:T(8,128)(2,1)S(1)}, bf16[8,1024]{1,0:T(8,128)(2,1)}, u32[]{:S(2)}) copy-start(bf16[8,1024]{1,0:T(8,128)(2,1)} %x_cols.1) | copy-start | bytes 49156
  1.3 0.7 %copy-start.5 = (s32[1,2]{1,0:T(1,128)S(1)}, s32[1,2]{1,0:T(1,128)}, u32[]{:S(2)}) copy-start(s32[1,2]{1,0:T(1,128)} %halo_ids.1) | copy-start | bytes 28
  17.1 11.4 %collective-permute-start.2 = (bf16[8,8,1152]{2,1,0:T(8,128)(2,1)S(1)}, bf16[8,8,1152]{2,1,0:T(8,128)(2,1)S(1)}, u32[]{:S(2)}, u32[]{:S(2)}) collective-permute-start(bf16[8,8,1152]{2,1,0:T(8,128)(2,1)S(1)} %all_to_all.10.xg.own), channel_id=1, source_target_pairs={{0,3},{1,2},{2,1},{3,0},{4,7},{5,6},{6,5},{7,4},{8,11},{9,10},{10,... | collective-permute-start | bytes 442376 | tf_op jit(solution)/shard_map/ppermute | solution.py:160
  17.1 11.4 %collective-permute-start.1 = (bf16[8,8,1152]{2,1,0:T(8,128)(2,1)S(1)}, bf16[8,8,1152]{2,1,0:T(8,128)(2,1)S(1)}, u32[]{:S(2)}, u32[]{:S(2)}) collective-permute-start(bf16[8,8,1152]{2,1,0:T(8,128)(2,1)S(1)} %all_to_all.10.xg.own), channel_id=1, source_target_pairs={{0,2},{1,3},{2,0},{3,1},{4,6},{5,7},{6,4},{7,5},{8,10},{9,11},{10,... | collective-permute-start | bytes 442376 | tf_op jit(solution)/shard_map/ppermute | solution.py:160
  18.7 9.9 %collective-permute-start = (bf16[8,8,1152]{2,1,0:T(8,128)(2,1)S(1)}, bf16[8,8,1152]{2,1,0:T(8,128)(2,1)S(1)}, u32[]{:S(2)}, u32[]{:S(2)}) collective-permute-start(bf16[8,8,1152]{2,1,0:T(8,128)(2,1)S(1)} %all_to_all.10.xg.own), channel_id=1, source_target_pairs={{0,1},{1,0},{2,3},{3,2},{4,5},{5,4},{6,7},{7,6},{8,9},{9,8},{10,11... | collective-permute-start | bytes 442376 | tf_op jit(solution)/shard_map/ppermute | solution.py:160
  19.0 1.6 %copy-start = (bf16[64,128,128]{2,1,0:T(8,128)(2,1)S(1)}, bf16[64,128,128]{2,1,0:T(8,128)(2,1)}, u32[]{:S(2)}) copy-start(bf16[64,128,128]{2,1,0:T(8,128)(2,1)} %a_tiles.1) | copy-start | bytes 6291460
  20.6 1.3 %copy-start.1 = (bf16[40,128,128]{2,1,0:T(8,128)(2,1)S(1)}, bf16[40,128,128]{2,1,0:T(8,128)(2,1)}, u32[]{:S(2)}) copy-start(bf16[40,128,128]{2,1,0:T(8,128)(2,1)} %q_tiles.1) | copy-start | bytes 3932164
  21.9 0.7 %copy-start.2 = (bf16[64,128]{1,0:T(8,128)(2,1)S(1)}, bf16[64,128]{1,0:T(8,128)(2,1)}, u32[]{:S(2)}) copy-start(bf16[64,128]{1,0:T(8,128)(2,1)} %precisions.1) | copy-start | bytes 49156
  22.6 0.7 %copy-start.4 = (s32[8,5]{1,0:T(8,128)S(1)}, s32[8,5]{1,0:T(8,128)}, u32[]{:S(2)}) copy-start(s32[8,5]{1,0:T(8,128)} %q_cols.1) | copy-start | bytes 484
  23.3 0.7 %copy-start.6 = (s32[64,1]{0,1:T(1,128)S(1)}, s32[64,1]{0,1:T(1,128)}, u32[]{:S(2)}) copy-start(s32[64,1]{0,1:T(1,128)} %param.14) | copy-start | bytes 772
  24.0 0.7 %copy-start.7 = (s32[64]{0:T(128)S(1)}, s32[64]{0:T(128)}, u32[]{:S(2)}) copy-start(s32[64]{0:T(128)} %subs.1) | copy-start | bytes 772

commit v2 on v1

v2 whole, which is shorter than its diff:
```python
import math

import jax
import jax.numpy as jnp
from jax import lax
from jax.experimental import pallas as pl
from jax.experimental.pallas import tpu as pltpu
from jax.sharding import PartitionSpec as P

OFFSETS = (-2, -1, 1, 2)
LANES = 128
NT = (((1,), (1,)), ((), ()))
UNROLL = 16
GRANT = 16 * 2**20


def offer_kernel(halo_ids, x_cols, offered, ids_here, ids_sem, x_sems):
    parts, cols, width = offered.shape
    nodes = width - LANES
    copies = [
        pltpu.make_async_copy(x_cols, offered.at[part, :, pl.ds(0, nodes)], x_sems.at[part])
        for part in range(parts)
    ]
    fetch = pltpu.make_async_copy(halo_ids, ids_here, ids_sem)
    fetch.start()
    for copy in copies:
        copy.start()
    fetch.wait()
    rows = lax.broadcasted_iota(jnp.int32, (cols, LANES), 0)
    ids = jnp.zeros((cols, LANES), jnp.float32)
    for j in range(halo_ids.shape[1]):
        ids = jnp.where(rows == j, ids_here[0, j].astype(jnp.float32), ids)
    ids = ids.astype(offered.dtype)
    for part in range(parts):
        offered[part, :, nodes:] = ids
    for copy in copies:
        copy.wait()


def project_kernel(
    owners, subs, q_cols, xg, a_tiles, precisions, q_tiles, weighted, prior, window
):
    parts, cols, width = xg.shape
    obs_count, tile, _ = a_tiles.shape
    row_blocks, neighbours = q_cols.shape
    nodes = row_blocks * tile
    halo = (window.shape[0] - row_blocks) // len(OFFSETS)
    me = lax.axis_index("mesh")

    for row in range(row_blocks):
        window[row] = xg[me, :, row * tile:(row + 1) * tile]
    for m, offset in enumerate(OFFSETS):
        part = lax.rem(me + offset + parts, parts)
        ids = xg[part, :, nodes:nodes + tile].astype(jnp.float32)
        for j in range(halo):
            wanted = jnp.broadcast_to(ids[j:j + 1, :], (cols, tile))
            picked = jnp.zeros((cols, tile), jnp.float32)
            for row in range(row_blocks):
                picked = jnp.where(
                    wanted == float(row),
                    xg[part, :, row * tile:(row + 1) * tile].astype(jnp.float32),
                    picked,
                )
            window[row_blocks + m * halo + j] = picked.astype(jnp.bfloat16)

    def project(step, carry):
        first = pl.multiple_of(step * UNROLL, UNROLL)
        scales = precisions[pl.ds(first, UNROLL), :].astype(jnp.float32)
        for u in range(UNROLL):
            t = step * UNROLL + u
            lanes = pl.ds(pl.multiple_of(subs[t] * tile, tile), tile)
            projected = lax.dot_general(
                xg[owners[t], :, lanes], a_tiles[t], NT, preferred_element_type=jnp.float32
            )
            weighted[t] = (scales[u:u + 1, :] * projected).astype(jnp.bfloat16)
        return carry

    lax.fori_loop(0, obs_count // UNROLL, project, 0)

    for row in range(row_blocks):
        total = None
        for k in range(neighbours):
            term = lax.dot_general(
                window[q_cols[row, k]], q_tiles[row * neighbours + k], NT,
                preferred_element_type=jnp.float32,
            )
            total = term if total is None else total + term
        prior[:, row * tile:(row + 1) * tile] = total


def spread_kernel(owners, subs, weighted, a_tiles, prior, summed):
    obs_count, tile, _ = a_tiles.shape
    summed[...] = jnp.zeros_like(summed)
    summed[lax.axis_index("mesh")] = prior[...]

    def spread(step, carry):
        made = [
            jnp.dot(weighted[step * UNROLL + u], a_tiles[step * UNROLL + u],
                    preferred_element_type=jnp.float32)
            for u in range(UNROLL)
        ]
        for u in range(UNROLL):
            t = step * UNROLL + u
            lanes = pl.ds(pl.multiple_of(subs[t] * tile, tile), tile)
            summed[owners[t], :, lanes] = summed[owners[t], :, lanes] + made[u]
        return carry

    lax.fori_loop(0, obs_count // UNROLL, spread, 0)


def over_parts(parts, step, carry):
    if parts > 16:
        return lax.fori_loop(0, parts, step, carry)
    for part in range(parts):
        carry = step(part, carry)
    return carry


def top_exponent(value):
    top = jnp.maximum(jnp.max(jnp.abs(value), axis=1, keepdims=True), 1e-30)
    return jnp.floor(jnp.log(32000.0 / top) * (1.0 / math.log(2.0)))


def power(exponent):
    return jnp.exp2(exponent)


def whole(value):
    return jnp.round(value).astype(jnp.int32).astype(jnp.int16)


def gram_kernel(summed, own, near1, near2, near3, message):
    parts, cols, nodes = summed.shape
    mine = lax.axis_index("col")

    def add(part, carry):
        value = summed[part]
        high = value.astype(jnp.bfloat16)
        low = (value - high.astype(jnp.float32)).astype(jnp.bfloat16)
        out = []
        for ref, old in zip((own, near1, near2, near3), carry):
            x = ref[part, :, :nodes]
            out.append(
                old
                + lax.dot_general(high, x, NT, preferred_element_type=jnp.float32)
                + lax.dot_general(low, x, NT, preferred_element_type=jnp.float32)
            )
        return tuple(out)

    pieces = over_parts(parts, add, (jnp.zeros((cols, cols), jnp.float32),) * 4)
    total = jnp.zeros((cols, LANES), jnp.float32)
    for k, piece in enumerate(pieces):
        wide = jnp.concatenate([piece, jnp.zeros((cols, LANES - cols), jnp.float32)], axis=1)
        total = total + pltpu.roll(wide, lax.bitwise_xor(mine, k) * cols, 1)

    quarter = LANES // 4
    lane = lax.broadcasted_iota(jnp.int32, (cols, LANES), 1)
    gram_exponent = top_exponent(total)
    scaled = total * power(gram_exponent)
    first = jnp.round(scaled)
    second = pltpu.roll((scaled - first) * 32768.0, quarter, 1)
    extra = jnp.where(lane < quarter, first, jnp.where(lane < 2 * quarter, second, gram_exponent))

    def put(part, carry):
        value = summed[part]
        exponent = top_exponent(value)
        message[part, :, :nodes] = whole(value * power(exponent))
        message[part, :, nodes:] = whole(jnp.where(lane < 3 * quarter, extra, exponent))
        return carry

    over_parts(parts, put, 0)


def collect_kernel(summed, arrived, product, gram):
    parts, cols, nodes = summed.shape
    quarter = LANES // 4
    me = lax.axis_index("mesh")

    def add(part, carry):
        total, pairs = carry
        extra = arrived[part, :, nodes:].astype(jnp.int32).astype(jnp.float32)
        back = power(-extra[:, 3 * quarter:3 * quarter + 1])
        here = arrived[part, :, :nodes].astype(jnp.int32).astype(jnp.float32) * back
        total = total + jnp.where(part == me, summed[part], here)
        values = extra + pltpu.roll(extra, LANES - quarter, 1) * (1.0 / 32768.0)
        return total, pairs + values * power(-extra[:, 2 * quarter:2 * quarter + 1])

    start = jnp.zeros((cols, nodes), jnp.float32), jnp.zeros((cols, LANES), jnp.float32)
    total, pairs = over_parts(parts, add, start)
    product[...] = total
    gram[...] = pairs[:, :gram.shape[1]] * (1.0 / math.sqrt(nodes * parts))


def body(x_cols, q_tiles, q_cols, halo_ids, a_tiles, obs_prec, tile_owner, tile_sub):
    cols, nodes = x_cols.shape
    parts, groups = lax.axis_size("mesh"), lax.axis_size("col")
    obs_count, tile, _ = a_tiles.shape
    row_blocks = nodes // tile
    halo = halo_ids.shape[1]
    width = nodes + LANES
    vmem, smem = pl.BlockSpec(memory_space=pltpu.VMEM), pl.BlockSpec(memory_space=pltpu.SMEM)
    hbm = pl.BlockSpec(memory_space=pltpu.HBM)
    offered = pl.pallas_call(
        offer_kernel,
        out_shape=jax.ShapeDtypeStruct((parts, cols, width), x_cols.dtype),
        in_specs=[hbm, hbm],
        out_specs=vmem,
        scratch_shapes=[
            pltpu.SMEM(halo_ids.shape, jnp.int32),
            pltpu.SemaphoreType.DMA,
            pltpu.SemaphoreType.DMA((parts,)),
        ],
        compiler_params=pltpu.CompilerParams(vmem_limit_bytes=GRANT),
        cost_estimate=pl.CostEstimate(
            flops=2_000_000_000, bytes_accessed=200_000, transcendentals=0
        ),
        name="offer",
    )(*(pltpu.with_memory_space_constraint(a, pltpu.HBM) for a in (halo_ids, x_cols)))
    xg = lax.all_to_all(offered, "mesh", 0, 0, tiled=True)
    def swap(array, k):
        return lax.ppermute(array, "col", [(i, i ^ k) for i in range(groups)])

    near2 = swap(xg, 2)
    near1 = swap(xg, 1)
    params = pltpu.CompilerParams(vmem_limit_bytes=GRANT)
    owners = tile_owner.reshape(-1)
    weighted, prior = pl.pallas_call(
        project_kernel,
        out_shape=[
            jax.ShapeDtypeStruct((obs_count, cols, tile), jnp.bfloat16),
            jax.ShapeDtypeStruct((cols, nodes), jnp.float32),
        ],
        in_specs=[smem, smem, smem, vmem, vmem, vmem, vmem],
        out_specs=[vmem, vmem],
        scratch_shapes=[pltpu.VMEM((row_blocks + len(OFFSETS) * halo, cols, tile), jnp.bfloat16)],
        compiler_params=params,
        cost_estimate=pl.CostEstimate(
            flops=60_000_000, bytes_accessed=4_000_000, transcendentals=0
        ),
        name="project",
    )(owners, tile_sub, q_cols, xg, a_tiles, obs_prec, q_tiles)
    near2, weighted = lax.optimization_barrier((near2, weighted))
    near3 = swap(near2, 1)
    summed = pl.pallas_call(
        spread_kernel,
        out_shape=jax.ShapeDtypeStruct((parts, cols, nodes), jnp.float32),
        in_specs=[smem, smem, vmem, vmem, vmem],
        out_specs=vmem,
        compiler_params=params,
        cost_estimate=pl.CostEstimate(
            flops=60_000_000, bytes_accessed=4_000_000, transcendentals=0
        ),
        name="spread",
    )(owners, tile_sub, weighted, a_tiles, prior)
    message = pl.pallas_call(
        gram_kernel,
        out_shape=jax.ShapeDtypeStruct((parts, cols, width), jnp.int16),
        in_specs=[vmem] * 5,
        out_specs=vmem,
        compiler_params=params,
        cost_estimate=pl.CostEstimate(
            flops=10_000_000, bytes_accessed=1_000_000, transcendentals=0
        ),
        name="gram",
    )(summed, xg, near1, near2, near3)
    arrived = lax.all_to_all(message, "mesh", 0, 0, tiled=True)
    product, gram = pl.pallas_call(
        collect_kernel,
        out_shape=[
            jax.ShapeDtypeStruct((cols, nodes), jnp.float32),
            jax.ShapeDtypeStruct((cols, groups * cols), jnp.float32),
        ],
        in_specs=[vmem, vmem],
        out_specs=[vmem, vmem],
        compiler_params=params,
        name="collect",
    )(summed, arrived)
    return product, gram.T


def solution(mesh):
    placed = (
        P("col", "mesh"),
        P("mesh", None, None),
        P("mesh", None),
        P("mesh", None),
        P("mesh", None, None),
        P("mesh", None),
        P("mesh", None),
        P("mesh"),
    )
    return jax.shard_map(
        body,
        mesh=mesh,
        in_specs=placed,
        out_specs=(P("col", "mesh"), P(None, "col")),
        check_vma=False,
    )
```

time: 44.6 us -> 35.8 us (0.80)
  local copies, waits for them, and re-layouts: 7.6 us -> 0.03 us
  blocking collectives: 27.9 us -> 25.1 us
  Pallas kernels: 5.49 us -> 7.44 us
  waiting for transfers between devices: 0.01 us -> 0.7 us
  other arithmetic: 0.62 us -> 0 us
    unnamed x16 -> x12, local copies, waits for them, and re-layouts: 6.98 us -> 0.03 us
    all_to_all x1, blocking collectives: 13.4 us -> 10.6 us  [body(): arrived = lax.all_to_all(message, 'mesh', 0, 0, tiled=True)]
    pallas_call x2 -> x4, Pallas kernels: 4.9 us -> 6.36 us  [the longest x1 2.88 us: body(): pl.pallas_call(project_kernel, out_shape=[jax.ShapeDtypeStruct((obs_count...]
    ppermute x3, waiting for transfers between devices: 0.01 us -> 0.7 us  [swap(): return lax.ppermute(array, 'col', [(i, i ^ k) for i in range(groups)])]
    slice x1 -> x0, local copies, waits for them, and re-layouts: 0.62 us -> none  [body(): return (summed[:, :nodes], gram)]
    div x1 -> x0, other arithmetic: 0.6 us -> none  [body(): gram = summed[:, nodes:nodes + groups * cols].T / math.sqrt(nodes * parts)]
    pallas_call x1, Pallas kernels: 0.59 us -> 1.09 us  [body(): pl.pallas_call(offer_kernel, out_shape=jax.ShapeDtypeStruct((parts, cols,...]
  transfers between devices with their start and end apart: 3 -> 3, of which waited for: 0 -> 1; matrix products, arithmetic and copies ran while one was open for 0% -> 0% of each run, Pallas kernels for 9% -> 13%
where the time goes in v2:
time: 35.8 us; the launch traced here: 35.5 us
  blocking collectives  25.1 us (70%)
  Pallas kernels  7.44 us (21%)
  starting transfers between devices  1.52 us (4%)
  between operations  0.74 us (2%)
  waiting for transfers between devices  0.7 us (2%)
    all_to_all x1, blocking collectives, body(): xg = lax.all_to_all(offered, 'mesh', 0, 0, tiled=True)  14.5 us
    all_to_all x1, blocking collectives, body(): arrived = lax.all_to_all(message, 'mesh', 0, 0, tiled=True)  10.6 us
    pallas_call x1, Pallas kernels, body(): pl.pallas_call(project_kernel, out_shape=[jax.ShapeDtypeStruct((obs_count...  2.88 us
    pallas_call x1, Pallas kernels, body(): pl.pallas_call(spread_kernel, out_shape=jax.ShapeDtypeStruct((parts, cols...  1.57 us
    ppermute x3, starting transfers between devices, swap(): return lax.ppermute(array, 'col', [(i, i ^ k) for i in range(groups)])  1.52 us
    pallas_call x1, Pallas kernels, body(): pl.pallas_call(gram_kernel, out_shape=jax.ShapeDtypeStruct((parts, cols,...  1.17 us
    pallas_call x1, Pallas kernels, body(): pl.pallas_call(offer_kernel, out_shape=jax.ShapeDtypeStruct((parts, cols,...  1.09 us
    pallas_call x1, Pallas kernels, body(): pl.pallas_call(collect_kernel, out_shape=[jax.ShapeDtypeStruct((cols, nod...  0.73 us
  transfers between devices with their start and end apart: 3, of which 1 were waited for; matrix products, arithmetic and copies ran while one was open for 0% of the time, Pallas kernels for 13%

profile of v2, /device:TPU:0, one launch (start us, length us, event | category | flops | bytes accessed | tf_op | source)
XLA Modules:
  0.0 35.5 jit_solution(6212217893117263464)
XLA Ops:
  0.6 0.0 copy-start.5
  0.6 0.0 copy-start
  0.7 0.0 copy-start.4
  0.7 0.0 copy-start.2
  0.7 0.0 copy-start.3
  0.7 0.0 copy-start.1
  0.7 1.1 %offer.1 = bf16[8,8,1152]{2,1,0:T(8,128)(2,1)S(1)} custom-call(s32[1,2]{1,0:T(1,128)} %halo_ids.1, bf16[8,1024]{1,0:T(8,128)(2,1)} %x_cols.1), custom_call_target="tpu_custom_call" | custom-call | flops 2000000000 | bytes 200000 | tf_op jit(solution)/shard_map/offer/pallas_call | solution.py:203
  1.8 14.5 %all_to_all.10.xg.own = bf16[8,8,1152]{2,1,0:T(8,128)(2,1)S(1)} all-to-all(bf16[8,8,1152]{2,1,0:T(8,128)(2,1)S(1)} %offer.1), channel_id=1, replica_groups=mesh['mesh'=8,'col'=4] {'mesh'}, dimensions={0} | all-to-all | bytes 294912 | tf_op jit(solution)/shard_map/all_to_all | solution.py:219
  16.3 1.5 %collective-permute-start = (bf16[8,8,1152]{2,1,0:T(8,128)(2,1)S(1)}, bf16[8,8,1152]{2,1,0:T(8,128)(2,1)S(1)}, u32[]{:S(2)}, u32[]{:S(2)}) collective-permute-start(bf16[8,8,1152]{2,1,0:T(8,128)(2,1)S(1)} %all_to_all.10.xg.own), channel_id=1, source_target_pairs={{0,2},{1,3},{2,0},{3,1},{4,6},{5,7},{6,4},{7,5},{8,10},{9,11},{10,... | collective-permute-start | bytes 442376 | tf_op jit(solution)/shard_map/ppermute | solution.py:221
  17.8 0.0 collective-permute-start.1
  17.8 0.0 copy-done.5
  17.8 0.0 copy-done
  17.9 0.0 copy-done.4
  17.9 0.0 copy-done.2
  17.9 0.0 copy-done.3
  17.9 0.0 copy-done.1
  17.9 2.9 %project.1 = (bf16[64,8,128]{2,1,0:T(8,128)(2,1)S(1)}, f32[8,1024]{1,0:T(8,128)S(1)}) custom-call(s32[64]{0:T(128)S(1)} %bitcast.2, s32[64]{0:T(128)S(1)} %copy-done.5, s32[8,5]{1,0:T(8,128)S(1)} %copy-done.3, bf16[8,8,1152]{2,1,0:T(8,128)(2,1)S(1)} %all_to_all.10.xg.own, bf16[64,128,128]{2,1,0:T(8,128)(2,1)S(1)} %copy-done, bf16[64,128]{1,0:T(8,128)(2,1)S(1)} %copy-done.2, ...), custom_call_target="tpu_custom_call" | custom-call | flops 60000000 | bytes 4000000 | tf_op jit(solution)/shard_map/project/pallas_call | solution.py:227
  20.8 0.7 %collective-permute-done.near2 = bf16[8,8,1152]{2,1,0:T(8,128)(2,1)S(1)} collective-permute-done((bf16[8,8,1152]{2,1,0:T(8,128)(2,1)S(1)}, bf16[8,8,1152]{2,1,0:T(8,128)(2,1)S(1)}, u32[]{:S(2)}, u32[]{:S(2)}) %collective-permute-start) | collective-permute-done | bytes 147488 | tf_op jit(solution)/shard_map/ppermute | solution.py:221
  21.5 0.0 collective-permute-start.2
  21.5 1.6 %spread.1.summed = f32[8,8,1024]{2,1,0:T(8,128)S(1)} custom-call(s32[64]{0:T(128)S(1)} %bitcast.3, s32[64]{0:T(128)S(1)} %copy-done.5, bf16[64,8,128]{2,1,0:T(8,128)(2,1)S(1)} %get-tuple-element.9.weighted, bf16[64,128,128]{2,1,0:T(8,128)(2,1)S(1)} %copy-done, f32[8,1024]{1,0:T(8,128)S(1)} %get-tuple-element.10.prior), custom_call_target="tpu_custom_call" | custom-call | flops 60000000 | bytes 4000000 | tf_op jit(solution)/shard_map/spread/pallas_call | solution.py:244
  23.0 0.0 collective-permute-done.1.near1
  23.0 0.0 collective-permute-done.2.near3
  23.1 1.2 %gram.1 = s16[8,8,1152]{2,1,0:T(8,128)(2,1)S(1)} custom-call(f32[8,8,1024]{2,1,0:T(8,128)S(1)} %spread.1.summed, bf16[8,8,1152]{2,1,0:T(8,128)(2,1)S(1)} %all_to_all.10.xg.own, bf16[8,8,1152]{2,1,0:T(8,128)(2,1)S(1)} %collective-permute-done.1.near1, bf16[8,8,1152]{2,1,0:T(8,128)(2,1)S(1)} %collective-permute-done.near2, ...), custom_call_target="tpu_custom_call" | custom-call | flops 10000000 | bytes 1000000 | tf_op jit(solution)/shard_map/gram/pallas_call | solution.py:255
  24.2 10.6 %all_to_all.11.arrived = s16[8,8,1152]{2,1,0:T(8,128)(2,1)S(1)} all-to-all(s16[8,8,1152]{2,1,0:T(8,128)(2,1)S(1)} %gram.1), channel_id=1, replica_groups=mesh['mesh'=8,'col'=4] {'mesh'}, dimensions={0} | all-to-all | bytes 294912 | tf_op jit(solution)/shard_map/all_to_all | solution.py:266
  34.8 0.7 %collect.1 = (f32[8,1024]{1,0:T(8,128)}, f32[8,32]{1,0:T(8,128)}) custom-call(f32[8,8,1024]{2,1,0:T(8,128)S(1)} %spread.1.summed, s16[8,8,1152]{2,1,0:T(8,128)(2,1)S(1)} %all_to_all.11.arrived), custom_call_target="tpu_custom_call" | custom-call | tf_op jit(solution)/shard_map/collect/pallas_call | solution.py:267
Async XLA Ops:
  0.6 17.2 %copy-start.5 = (s32[64]{0:T(128)S(1)}, s32[64]{0:T(128)}, u32[]{:S(2)}) copy-start(s32[64]{0:T(128)} %subs.3) | copy-start | bytes 772
  0.6 17.2 %copy-start = (bf16[64,128,128]{2,1,0:T(8,128)(2,1)S(1)}, bf16[64,128,128]{2,1,0:T(8,128)(2,1)}, u32[]{:S(2)}) copy-start(bf16[64,128,128]{2,1,0:T(8,128)(2,1)} %a_tiles.3) | copy-start | bytes 6291460
  0.7 17.2 %copy-start.4 = (s32[64,1]{0,1:T(1,128)S(1)}, s32[64,1]{0,1:T(1,128)}, u32[]{:S(2)}) copy-start(s32[64,1]{0,1:T(1,128)} %param.14) | copy-start | bytes 772
  0.7 17.2 %copy-start.2 = (bf16[64,128]{1,0:T(8,128)(2,1)S(1)}, bf16[64,128]{1,0:T(8,128)(2,1)}, u32[]{:S(2)}) copy-start(bf16[64,128]{1,0:T(8,128)(2,1)} %precisions.1) | copy-start | bytes 49156
  0.7 17.2 %copy-start.3 = (s32[8,5]{1,0:T(8,128)S(1)}, s32[8,5]{1,0:T(8,128)}, u32[]{:S(2)}) copy-start(s32[8,5]{1,0:T(8,128)} %q_cols.1) | copy-start | bytes 484
  0.7 17.2 %copy-start.1 = (bf16[40,128,128]{2,1,0:T(8,128)(2,1)S(1)}, bf16[40,128,128]{2,1,0:T(8,128)(2,1)}, u32[]{:S(2)}) copy-start(bf16[40,128,128]{2,1,0:T(8,128)(2,1)} %q_tiles.1) | copy-start | bytes 3932164
  16.3 5.1 %collective-permute-start = (bf16[8,8,1152]{2,1,0:T(8,128)(2,1)S(1)}, bf16[8,8,1152]{2,1,0:T(8,128)(2,1)S(1)}, u32[]{:S(2)}, u32[]{:S(2)}) collective-permute-start(bf16[8,8,1152]{2,1,0:T(8,128)(2,1)S(1)} %all_to_all.10.xg.own), channel_id=1, source_target_pairs={{0,2},{1,3},{2,0},{3,1},{4,6},{5,7},{6,4},{7,5},{8,10},{9,11},{10,... | collective-permute-start | bytes 442376 | tf_op jit(solution)/shard_map/ppermute | solution.py:221
  17.8 5.2 %collective-permute-start.1 = (bf16[8,8,1152]{2,1,0:T(8,128)(2,1)S(1)}, bf16[8,8,1152]{2,1,0:T(8,128)(2,1)S(1)}, u32[]{:S(2)}, u32[]{:S(2)}) collective-permute-start(bf16[8,8,1152]{2,1,0:T(8,128)(2,1)S(1)} %all_to_all.10.xg.own), channel_id=1, source_target_pairs={{0,1},{1,0},{2,3},{3,2},{4,5},{5,4},{6,7},{7,6},{8,9},{9,8},{10,11... | collective-permute-start | bytes 442376 | tf_op jit(solution)/shard_map/ppermute | solution.py:221
  21.5 1.6 %collective-permute-start.2 = (bf16[8,8,1152]{2,1,0:T(8,128)(2,1)S(1)}, bf16[8,8,1152]{2,1,0:T(8,128)(2,1)S(1)}, u32[]{:S(2)}, u32[]{:S(2)}) collective-permute-start(bf16[8,8,1152]{2,1,0:T(8,128)(2,1)S(1)} %collective-permute-done.near2), channel_id=1, source_target_pairs={{0,1},{1,0},{2,3},{3,2},{4,5},{5,4},{6,7},{7,6},{8,9},{9,8},{10,11... | collective-permute-start | bytes 442376 | tf_op jit(solution)/shard_map/ppermute | solution.py:221

commit v3 on v2

--- a/solution.py
+++ b/solution.py
@@ -10,22 +10,18 @@
 OFFSETS = (-2, -1, 1, 2)
 LANES = 128
 NT = (((1,), (1,)), ((), ()))
-UNROLL = 16
+UNROLL = 64
 GRANT = 16 * 2**20
 
 
-def offer_kernel(halo_ids, x_cols, offered, ids_here, ids_sem, x_sems):
+def offer_kernel(halo_ids, x_cols, offered, ids_here, x_here, sems):
     parts, cols, width = offered.shape
     nodes = width - LANES
-    copies = [
-        pltpu.make_async_copy(x_cols, offered.at[part, :, pl.ds(0, nodes)], x_sems.at[part])
-        for part in range(parts)
-    ]
-    fetch = pltpu.make_async_copy(halo_ids, ids_here, ids_sem)
-    fetch.start()
-    for copy in copies:
-        copy.start()
-    fetch.wait()
+    fetch_ids = pltpu.make_async_copy(halo_ids, ids_here, sems.at[0])
+    fetch_x = pltpu.make_async_copy(x_cols, x_here, sems.at[1])
+    fetch_ids.start()
+    fetch_x.start()
+    fetch_ids.wait()
     rows = lax.broadcasted_iota(jnp.int32, (cols, LANES), 0)
     ids = jnp.zeros((cols, LANES), jnp.float32)
     for j in range(halo_ids.shape[1]):
@@ -33,12 +29,14 @@
     ids = ids.astype(offered.dtype)
     for part in range(parts):
         offered[part, :, nodes:] = ids
-    for copy in copies:
-        copy.wait()
-
-
-def project_kernel(
-    owners, subs, q_cols, xg, a_tiles, precisions, q_tiles, weighted, prior, window
+    fetch_x.wait()
+    own = x_here[...]
+    for part in range(parts):
+        offered[part, :, :nodes] = own
+
+
+def terms_kernel(
+    owners, subs, q_cols, xg, a_tiles, precisions, q_tiles, summed, window, weighted
 ):
     parts, cols, width = xg.shape
     obs_count, tile, _ = a_tiles.shape
@@ -46,6 +44,29 @@
     nodes = row_blocks * tile
     halo = (window.shape[0] - row_blocks) // len(OFFSETS)
     me = lax.axis_index("mesh")
+    unroll = math.gcd(obs_count, UNROLL)
+
+    def lanes_of(t):
+        return pl.ds(pl.multiple_of(subs[t] * tile, tile), tile)
+
+    def steps(step):
+        if obs_count == unroll:
+            step(0)
+        else:
+            pl.loop(0, obs_count // unroll)(step)
+
+    summed[...] = jnp.zeros_like(summed)
+
+    @steps
+    def project(step):
+        first = step * unroll
+        scales = precisions[pl.ds(first, unroll), :].astype(jnp.float32)
+        for u in range(unroll):
+            t = first + u
+            projected = lax.dot_general(
+                xg[owners[t], :, lanes_of(t)], a_tiles[t], NT, preferred_element_type=jnp.float32
+            )
+            weighted[t] = (scales[u:u + 1, :] * projected).astype(jnp.bfloat16)
 
     for row in range(row_blocks):
         window[row] = xg[me, :, row * tile:(row + 1) * tile]
@@ -63,20 +84,6 @@
                 )
             window[row_blocks + m * halo + j] = picked.astype(jnp.bfloat16)
 
-    def project(step, carry):
-        first = pl.multiple_of(step * UNROLL, UNROLL)
-        scales = precisions[pl.ds(first, UNROLL), :].astype(jnp.float32)
-        for u in range(UNROLL):
-            t = step * UNROLL + u
-            lanes = pl.ds(pl.multiple_of(subs[t] * tile, tile), tile)
-            projected = lax.dot_general(
-                xg[owners[t], :, lanes], a_tiles[t], NT, preferred_element_type=jnp.float32
-            )
-            weighted[t] = (scales[u:u + 1, :] * projected).astype(jnp.bfloat16)
-        return carry
-
-    lax.fori_loop(0, obs_count // UNROLL, project, 0)
-
     for row in range(row_blocks):
         total = None
         for k in range(neighbours):
@@ -85,27 +92,18 @@
                 preferred_element_type=jnp.float32,
             )
             total = term if total is None else total + term
-        prior[:, row * tile:(row + 1) * tile] = total
-
-
-def spread_kernel(owners, subs, weighted, a_tiles, prior, summed):
-    obs_count, tile, _ = a_tiles.shape
-    summed[...] = jnp.zeros_like(summed)
-    summed[lax.axis_index("mesh")] = prior[...]
-
-    def spread(step, carry):
+        summed[me, :, row * tile:(row + 1) * tile] = total
+
+    @steps
+    def spread(step):
+        first = step * unroll
         made = [
-            jnp.dot(weighted[step * UNROLL + u], a_tiles[step * UNROLL + u],
-                    preferred_element_type=jnp.float32)
-            for u in range(UNROLL)
+            jnp.dot(weighted[first + u], a_tiles[first + u], preferred_element_type=jnp.float32)
+            for u in range(unroll)
         ]
-        for u in range(UNROLL):
-            t = step * UNROLL + u
-            lanes = pl.ds(pl.multiple_of(subs[t] * tile, tile), tile)
-            summed[owners[t], :, lanes] = summed[owners[t], :, lanes] + made[u]
-        return carry
-
-    lax.fori_loop(0, obs_count // UNROLL, spread, 0)
+        for u in range(unroll):
+            t = first + u
+            summed[owners[t], :, lanes_of(t)] = summed[owners[t], :, lanes_of(t)] + made[u]
 
 
 def over_parts(parts, step, carry):
@@ -129,16 +127,15 @@
     return jnp.round(value).astype(jnp.int32).astype(jnp.int16)
 
 
-def gram_kernel(summed, own, near1, near2, near3, message):
+def pair_products(summed, near, carry):
     parts, cols, nodes = summed.shape
-    mine = lax.axis_index("col")
 
     def add(part, carry):
         value = summed[part]
         high = value.astype(jnp.bfloat16)
         low = (value - high.astype(jnp.float32)).astype(jnp.bfloat16)
         out = []
-        for ref, old in zip((own, near1, near2, near3), carry):
+        for ref, old in zip(near, carry):
             x = ref[part, :, :nodes]
             out.append(
                 old
@@ -147,12 +144,35 @@
             )
         return tuple(out)
 
-    pieces = over_parts(parts, add, (jnp.zeros((cols, cols), jnp.float32),) * 4)
-    total = jnp.zeros((cols, LANES), jnp.float32)
-    for k, piece in enumerate(pieces):
-        wide = jnp.concatenate([piece, jnp.zeros((cols, LANES - cols), jnp.float32)], axis=1)
-        total = total + pltpu.roll(wide, lax.bitwise_xor(mine, k) * cols, 1)
-
+    return over_parts(parts, add, carry)
+
+
+def at_column(piece, k):
+    cols = piece.shape[0]
+    wide = jnp.concatenate([piece, jnp.zeros((cols, LANES - cols), jnp.float32)], axis=1)
+    return pltpu.roll(wide, lax.bitwise_xor(lax.axis_index("col"), k) * cols, 1)
+
+
+def code_kernel(summed, near0, near1, near2, message, pairs, exponents):
+    parts, cols, nodes = summed.shape
+
+    def put(part, carry):
+        value = summed[part]
+        exponent = top_exponent(value)
+        message[part, :, :nodes] = whole(value * power(exponent))
+        exponents[part] = jnp.broadcast_to(exponent, (cols, LANES))
+        return carry
+
+    over_parts(parts, put, 0)
+    zero = jnp.zeros((cols, cols), jnp.float32)
+    pieces = pair_products(summed, (near0, near1, near2), (zero, zero, zero))
+    pairs[...] = at_column(pieces[0], 0) + at_column(pieces[1], 1) + at_column(pieces[2], 2)
+
+
+def gram_kernel(coded, pairs, exponents, summed, near3, message):
+    parts, cols, nodes = summed.shape
+    (piece,) = pair_products(summed, (near3,), (jnp.zeros((cols, cols), jnp.float32),))
+    total = pairs[...] + at_column(piece, 3)
     quarter = LANES // 4
     lane = lax.broadcasted_iota(jnp.int32, (cols, LANES), 1)
     gram_exponent = top_exponent(total)
@@ -162,10 +182,7 @@
     extra = jnp.where(lane < quarter, first, jnp.where(lane < 2 * quarter, second, gram_exponent))
 
     def put(part, carry):
-        value = summed[part]
-        exponent = top_exponent(value)
-        message[part, :, :nodes] = whole(value * power(exponent))
-        message[part, :, nodes:] = whole(jnp.where(lane < 3 * quarter, extra, exponent))
+        message[part, :, nodes:] = whole(jnp.where(lane < 3 * quarter, extra, exponents[part]))
         return carry
 
     over_parts(parts, put, 0)
@@ -207,8 +224,8 @@
         out_specs=vmem,
         scratch_shapes=[
             pltpu.SMEM(halo_ids.shape, jnp.int32),
-            pltpu.SemaphoreType.DMA,
-            pltpu.SemaphoreType.DMA((parts,)),
+            pltpu.VMEM(x_cols.shape, x_cols.dtype),
+            pltpu.SemaphoreType.DMA((2,)),
         ],
         compiler_params=pltpu.CompilerParams(vmem_limit_bytes=GRANT),
         cost_estimate=pl.CostEstimate(
@@ -224,45 +241,51 @@
     near1 = swap(xg, 1)
     params = pltpu.CompilerParams(vmem_limit_bytes=GRANT)
     owners = tile_owner.reshape(-1)
-    weighted, prior = pl.pallas_call(
-        project_kernel,
-        out_shape=[
-            jax.ShapeDtypeStruct((obs_count, cols, tile), jnp.bfloat16),
-            jax.ShapeDtypeStruct((cols, nodes), jnp.float32),
+    summed = pl.pallas_call(
+        terms_kernel,
+        out_shape=jax.ShapeDtypeStruct((parts, cols, nodes), jnp.float32),
+        in_specs=[smem, smem, smem, vmem, vmem, vmem, vmem],
+        out_specs=vmem,
+        scratch_shapes=[
+            pltpu.VMEM((row_blocks + len(OFFSETS) * halo, cols, tile), jnp.bfloat16),
+            pltpu.VMEM((obs_count, cols, tile), jnp.bfloat16),
         ],
-        in_specs=[smem, smem, smem, vmem, vmem, vmem, vmem],
-        out_specs=[vmem, vmem],
-        scratch_shapes=[pltpu.VMEM((row_blocks + len(OFFSETS) * halo, cols, tile), jnp.bfloat16)],
         compiler_params=params,
         cost_estimate=pl.CostEstimate(
-            flops=60_000_000, bytes_accessed=4_000_000, transcendentals=0
+            flops=100_000_000, bytes_accessed=4_000_000, transcendentals=0
         ),
-        name="project",
+        name="terms",
     )(owners, tile_sub, q_cols, xg, a_tiles, obs_prec, q_tiles)
-    near2, weighted = lax.optimization_barrier((near2, weighted))
+    near2, summed = lax.optimization_barrier((near2, summed))
     near3 = swap(near2, 1)
-    summed = pl.pallas_call(
-        spread_kernel,
-        out_shape=jax.ShapeDtypeStruct((parts, cols, nodes), jnp.float32),
-        in_specs=[smem, smem, vmem, vmem, vmem],
-        out_specs=vmem,
+    message_type = jax.ShapeDtypeStruct((parts, cols, width), jnp.int16)
+    coded, pairs, exponents = pl.pallas_call(
+        code_kernel,
+        out_shape=[
+            message_type,
+            jax.ShapeDtypeStruct((cols, LANES), jnp.float32),
+            jax.ShapeDtypeStruct((parts, cols, LANES), jnp.float32),
+        ],
+        in_specs=[vmem] * 4,
+        out_specs=[vmem] * 3,
         compiler_params=params,
         cost_estimate=pl.CostEstimate(
-            flops=60_000_000, bytes_accessed=4_000_000, transcendentals=0
+            flops=30_000_000, bytes_accessed=1_000_000, transcendentals=0
         ),
-        name="spread",
-    )(owners, tile_sub, weighted, a_tiles, prior)
+        name="code",
+    )(summed, xg, near1, near2)
     message = pl.pallas_call(
         gram_kernel,
-        out_shape=jax.ShapeDtypeStruct((parts, cols, width), jnp.int16),
-        in_specs=[vmem] * 5,
+        out_shape=message_type,
+        in_specs=[pl.BlockSpec(memory_space=pl.ANY)] + [vmem] * 4,
         out_specs=vmem,
+        input_output_aliases={0: 0},
         compiler_params=params,
         cost_estimate=pl.CostEstimate(
             flops=10_000_000, bytes_accessed=1_000_000, transcendentals=0
         ),
         name="gram",
-    )(summed, xg, near1, near2, near3)
+    )(coded, pairs, exponents, summed, near3)
     arrived = lax.all_to_all(message, "mesh", 0, 0, tiled=True)
     product, gram = pl.pallas_call(
         collect_kernel,

time: 35.8 us -> 34.6 us (0.966)
  Pallas kernels: 7.44 us -> 6 us
  waiting for transfers between devices: 0.7 us -> 1.08 us
    pallas_call x3, Pallas kernels: 5.63 us -> 4.38 us  [the longest x1 3.03 us: body(): pl.pallas_call(terms_kernel, out_shape=jax.ShapeDtypeStruct((parts, cols,...]
    ppermute x3, waiting for transfers between devices: 0.7 us -> 1.08 us  [swap(): return lax.ppermute(array, 'col', [(i, i ^ k) for i in range(groups)])]
  transfers between devices with their start and end apart: 3 -> 3, of which waited for: 1 -> 2; matrix products, arithmetic and copies ran while one was open for 0% -> 0% of each run, Pallas kernels for 13% -> 11%
where the time goes in v3:
time: 34.6 us; the launch traced here: 34.3 us
  blocking collectives  24.9 us (72%)
  Pallas kernels  6 us (17%)
  starting transfers between devices  1.55 us (4%)
  waiting for transfers between devices  1.08 us (3%)
  between operations  0.73 us (2%)
    all_to_all x1, blocking collectives, body(): xg = lax.all_to_all(offered, 'mesh', 0, 0, tiled=True)  14.7 us
    all_to_all x1, blocking collectives, body(): arrived = lax.all_to_all(message, 'mesh', 0, 0, tiled=True)  10.2 us
    pallas_call x1, Pallas kernels, body(): pl.pallas_call(terms_kernel, out_shape=jax.ShapeDtypeStruct((parts, cols,...  3.03 us
    ppermute x3, starting transfers between devices, swap(): return lax.ppermute(array, 'col', [(i, i ^ k) for i in range(groups)])  1.55 us
    ppermute x3, waiting for transfers between devices, swap(): return lax.ppermute(array, 'col', [(i, i ^ k) for i in range(groups)])  1.08 us
    pallas_call x1, Pallas kernels, body(): pl.pallas_call(offer_kernel, out_shape=jax.ShapeDtypeStruct((parts, cols,...  0.89 us
    pallas_call x1, Pallas kernels, body(): pl.pallas_call(code_kernel, out_shape=[message_type, jax.ShapeDtypeStruct...  0.81 us
    pallas_call x1, Pallas kernels, body(): pl.pallas_call(collect_kernel, out_shape=[jax.ShapeDtypeStruct((cols, nod...  0.73 us
  transfers between devices with their start and end apart: 3, of which 2 were waited for; matrix products, arithmetic and copies ran while one was open for 0% of the time, Pallas kernels for 11%

profile of v3, /device:TPU:0, one launch (start us, length us, event | category | flops | bytes accessed | tf_op | source)
XLA Modules:
  0.0 34.3 jit_solution(4041469860733178746)
XLA Ops:
  0.6 0.0 copy-start.5
  0.6 0.0 copy-start.4
  0.7 0.0 copy-start.2
  0.7 0.0 copy-start
  0.7 0.0 copy-start.3
  0.7 0.0 copy-start.1
  0.7 0.9 %offer.1 = bf16[8,8,1152]{2,1,0:T(8,128)(2,1)S(1)} custom-call(s32[1,2]{1,0:T(1,128)} %halo_ids.1, bf16[8,1024]{1,0:T(8,128)(2,1)} %x_cols.1), custom_call_target="tpu_custom_call" | custom-call | flops 2000000000 | bytes 200000 | tf_op jit(solution)/shard_map/offer/pallas_call | solution.py:220
  1.6 14.7 %all_to_all.10.xg.near0 = bf16[8,8,1152]{2,1,0:T(8,128)(2,1)S(1)} all-to-all(bf16[8,8,1152]{2,1,0:T(8,128)(2,1)S(1)} %offer.1), channel_id=1, replica_groups=mesh['mesh'=8,'col'=4] {'mesh'}, dimensions={0} | all-to-all | bytes 294912 | tf_op jit(solution)/shard_map/all_to_all | solution.py:236
  16.3 1.5 %collective-permute-start = (bf16[8,8,1152]{2,1,0:T(8,128)(2,1)S(1)}, bf16[8,8,1152]{2,1,0:T(8,128)(2,1)S(1)}, u32[]{:S(2)}, u32[]{:S(2)}) collective-permute-start(bf16[8,8,1152]{2,1,0:T(8,128)(2,1)S(1)} %all_to_all.10.xg.near0), channel_id=1, source_target_pairs={{0,2},{1,3},{2,0},{3,1},{4,6},{5,7},{6,4},{7,5},{8,10},{9,11},{10,... | collective-permute-start | bytes 442376 | tf_op jit(solution)/shard_map/ppermute | solution.py:238
  17.8 0.0 collective-permute-start.1
  17.8 0.0 copy-done.5
  17.8 0.0 copy-done.4
  17.8 0.0 copy-done.2
  17.8 0.0 copy-done
  17.8 0.0 copy-done.3
  17.8 0.0 copy-done.1
  17.8 3.0 %terms.1.summed = f32[8,8,1024]{2,1,0:T(8,128)S(1)} custom-call(s32[64]{0:T(128)S(1)} %bitcast.2, s32[64]{0:T(128)S(1)} %copy-done.5, s32[8,5]{1,0:T(8,128)S(1)} %copy-done.3, bf16[8,8,1152]{2,1,0:T(8,128)(2,1)S(1)} %all_to_all.10.xg.near0, bf16[64,128,128]{2,1,0:T(8,128)(2,1)S(1)} %copy-done, bf16[64,128]{1,0:T(8,128)(2,1)S(1)} %copy-done.2, ...), custom_call_target="tpu_custom_call" | custom-call | flops 100000000 | bytes 4000000 | tf_op jit(solution)/shard_map/terms/pallas_call | solution.py:244
  20.9 0.5 %collective-permute-done.near2 = bf16[8,8,1152]{2,1,0:T(8,128)(2,1)S(1)} collective-permute-done((bf16[8,8,1152]{2,1,0:T(8,128)(2,1)S(1)}, bf16[8,8,1152]{2,1,0:T(8,128)(2,1)S(1)}, u32[]{:S(2)}, u32[]{:S(2)}) %collective-permute-start) | collective-permute-done | bytes 147488 | tf_op jit(solution)/shard_map/ppermute | solution.py:238
  21.4 0.0 collective-permute-start.2
  21.4 0.0 collective-permute-done.1.near1
  21.4 0.8 %code.1 = (s16[8,8,1152]{2,1,0:T(8,128)(2,1)S(1)}, f32[8,128]{1,0:T(8,128)S(1)}, f32[8,8,128]{2,1,0:T(8,128)S(1)}) custom-call(f32[8,8,1024]{2,1,0:T(8,128)S(1)} %terms.1.summed, bf16[8,8,1152]{2,1,0:T(8,128)(2,1)S(1)} %all_to_all.10.xg.near0, bf16[8,8,1152]{2,1,0:T(8,128)(2,1)S(1)} %collective-permute-done.1.near1, ...), custom_call_target="tpu_custom_call" | custom-call | flops 30000000 | bytes 1000000 | tf_op jit(solution)/shard_map/code/pallas_call | solution.py:262
  22.2 0.5 %collective-permute-done.2.near3 = bf16[8,8,1152]{2,1,0:T(8,128)(2,1)S(1)} collective-permute-done((bf16[8,8,1152]{2,1,0:T(8,128)(2,1)S(1)}, bf16[8,8,1152]{2,1,0:T(8,128)(2,1)S(1)}, u32[]{:S(2)}, u32[]{:S(2)}) %collective-permute-start.2) | collective-permute-done | bytes 147488 | tf_op jit(solution)/shard_map/ppermute | solution.py:238
  22.8 0.5 %gram.1 = s16[8,8,1152]{2,1,0:T(8,128)(2,1)S(1)} custom-call(s16[8,8,1152]{2,1,0:T(8,128)(2,1)S(1)} %get-tuple-element.11.coded, f32[8,128]{1,0:T(8,128)S(1)} %get-tuple-element.12.pairs, f32[8,8,128]{2,1,0:T(8,128)S(1)} %get-tuple-element.13.exponents, f32[8,8,1024]{2,1,0:T(8,128)S(1)} %terms.1.summed, ...), custom_call_target="tpu_custom_call", output_to_operand_aliasing={{}: (0, {})} | custom-call | flops 10000000 | bytes 1000000 | tf_op jit(solution)/shard_map/gram/pallas_call | solution.py:277
  23.3 10.2 %all_to_all.11.arrived = s16[8,8,1152]{2,1,0:T(8,128)(2,1)S(1)} all-to-all(s16[8,8,1152]{2,1,0:T(8,128)(2,1)S(1)} %gram.1), channel_id=1, replica_groups=mesh['mesh'=8,'col'=4] {'mesh'}, dimensions={0} | all-to-all | bytes 294912 | tf_op jit(solution)/shard_map/all_to_all | solution.py:289
  33.5 0.7 %collect.1 = (f32[8,1024]{1,0:T(8,128)}, f32[8,32]{1,0:T(8,128)}) custom-call(f32[8,8,1024]{2,1,0:T(8,128)S(1)} %terms.1.summed, s16[8,8,1152]{2,1,0:T(8,128)(2,1)S(1)} %all_to_all.11.arrived), custom_call_target="tpu_custom_call" | custom-call | tf_op jit(solution)/shard_map/collect/pallas_call | solution.py:290
Async XLA Ops:
  0.6 17.2 %copy-start.5 = (s32[64]{0:T(128)S(1)}, s32[64]{0:T(128)}, u32[]{:S(2)}) copy-start(s32[64]{0:T(128)} %subs.1) | copy-start | bytes 772
  0.6 17.1 %copy-start.4 = (s32[64,1]{0,1:T(1,128)S(1)}, s32[64,1]{0,1:T(1,128)}, u32[]{:S(2)}) copy-start(s32[64,1]{0,1:T(1,128)} %param.14) | copy-start | bytes 772
  0.7 17.1 %copy-start.2 = (bf16[64,128]{1,0:T(8,128)(2,1)S(1)}, bf16[64,128]{1,0:T(8,128)(2,1)}, u32[]{:S(2)}) copy-start(bf16[64,128]{1,0:T(8,128)(2,1)} %precisions.1) | copy-start | bytes 49156
  0.7 17.1 %copy-start = (bf16[64,128,128]{2,1,0:T(8,128)(2,1)S(1)}, bf16[64,128,128]{2,1,0:T(8,128)(2,1)}, u32[]{:S(2)}) copy-start(bf16[64,128,128]{2,1,0:T(8,128)(2,1)} %a_tiles.1) | copy-start | bytes 6291460
  0.7 17.1 %copy-start.3 = (s32[8,5]{1,0:T(8,128)S(1)}, s32[8,5]{1,0:T(8,128)}, u32[]{:S(2)}) copy-start(s32[8,5]{1,0:T(8,128)} %q_cols.1) | copy-start | bytes 484
  0.7 17.1 %copy-start.1 = (bf16[40,128,128]{2,1,0:T(8,128)(2,1)S(1)}, bf16[40,128,128]{2,1,0:T(8,128)(2,1)}, u32[]{:S(2)}) copy-start(bf16[40,128,128]{2,1,0:T(8,128)(2,1)} %q_tiles.1) | copy-start | bytes 3932164
  16.3 5.1 %collective-permute-start = (bf16[8,8,1152]{2,1,0:T(8,128)(2,1)S(1)}, bf16[8,8,1152]{2,1,0:T(8,128)(2,1)S(1)}, u32[]{:S(2)}, u32[]{:S(2)}) collective-permute-start(bf16[8,8,1152]{2,1,0:T(8,128)(2,1)S(1)} %all_to_all.10.xg.near0), channel_id=1, source_target_pairs={{0,2},{1,3},{2,0},{3,1},{4,6},{5,7},{6,4},{7,5},{8,10},{9,11},{10,... | collective-permute-start | bytes 442376 | tf_op jit(solution)/shard_map/ppermute | solution.py:238
  17.8 3.7 %collective-permute-start.1 = (bf16[8,8,1152]{2,1,0:T(8,128)(2,1)S(1)}, bf16[8,8,1152]{2,1,0:T(8,128)(2,1)S(1)}, u32[]{:S(2)}, u32[]{:S(2)}) collective-permute-start(bf16[8,8,1152]{2,1,0:T(8,128)(2,1)S(1)} %all_to_all.10.xg.near0), channel_id=1, source_target_pairs={{0,1},{1,0},{2,3},{3,2},{4,5},{5,4},{6,7},{7,6},{8,9},{9,8},{10,11... | collective-permute-start | bytes 442376 | tf_op jit(solution)/shard_map/ppermute | solution.py:238
  21.4 1.4 %collective-permute-start.2 = (bf16[8,8,1152]{2,1,0:T(8,128)(2,1)S(1)}, bf16[8,8,1152]{2,1,0:T(8,128)(2,1)S(1)}, u32[]{:S(2)}, u32[]{:S(2)}) collective-permute-start(bf16[8,8,1152]{2,1,0:T(8,128)(2,1)S(1)} %collective-permute-done.near2), channel_id=1, source_target_pairs={{0,1},{1,0},{2,3},{3,2},{4,5},{5,4},{6,7},{7,6},{8,9},{9,8},{10,11... | collective-permute-start | bytes 442376 | tf_op jit(solution)/shard_map/ppermute | solution.py:238
